TPU v7x, 32 devices: a whole 2x2x4 slice. The times are simulated.
32 devices in a mesh: ctx: 16 (over z, y, x), head: 2 (over core).
Axes of the slice: x: 2, y: 2, z: 4, core: 2. Of those that a mesh axis runs over, the one named last changes fastest.
Arguments:
- q_heads: bfloat16 [32, 24576], P('ctx', 'head'), may hold values from -6 to 6
- w_uk: bfloat16 [128, 128, 512], P('head'), may hold values from -1 to 1
- latent_t: bfloat16 [576, 16384], P(None, 'ctx'), may hold values from -48 to 48
- index_query: bfloat16 [32, 8192], P('ctx', 'head'), may hold values from -48 to 48
- index_key: bfloat16 [16384, 128], P('ctx'), may hold values from -4 to 4
- head_weight: bfloat16 [32, 64], P('ctx', 'head'), may hold values from 0.099609375 to 1
- query_pos: int32 [32], replicated, may hold values from 8192 to 16383
- key_start: int32 [32], replicated, may hold values from 0 to 4095
Outputs:
- grad_index_query: float32 [32, 8192], P('ctx', 'head')
- grad_index_key: float32 [16384, 128], P('ctx')
- grad_head_weight: float32 [32, 64], P('ctx', 'head')
All inputs are finite; a program needn't handle non-finite values.
Results may differ from a plain program's by a relative error of at most 0.0035.
Values may be sent and summed in bfloat16 or wider, within the bound.
No kernel may reach another device: no remote copies, remote signals or barrier semaphores. Data moves between devices by JAX's collectives and lax.ppermute only.
A program may use at most 192 MiB of HBM per device.

v0:
```python
import functools
import math

import jax
import jax.numpy as jnp
from jax import lax
from jax.experimental import pallas as pl
from jax.experimental.pallas import tpu as pltpu
from jax.sharding import PartitionSpec as P


MLA_HEADS = 128
ROPE_DIM = 64
NOPE_DIM = 128
INDEX_HEADS = 64
INDEX_DIM = 128
WIDTH = NOPE_DIM + ROPE_DIM
LANES = 128


MASKED = -1e30
HEADS_A_STEP = 8
LOG2E = math.log2(math.e)
f32 = jnp.float32
bf16 = jnp.bfloat16
HBM_WHOLE = pl.BlockSpec(memory_space=pltpu.HBM)
VMEM_WHOLE = pl.BlockSpec(memory_space=pltpu.VMEM)
SMEM_WHOLE = pl.BlockSpec(memory_space=pltpu.SMEM)


def exchange_stages(size):
    bits = size.bit_length() - 1
    stages = []
    while bits > 0:
        take = 2 if bits >= 2 else 1
        bits -= take
        stages.append([k << bits for k in range(1 << take)])
    return stages


def send(block, axis, size, mask):
    return lax.ppermute(block, axis, [(i, i ^ mask) for i in range(size)])


def gather_pieces(own, axis, size):
    *stages, last = exchange_stages(size)
    early = [send(own, axis, size, mask) for mask in last[1:]]
    blocks, offsets = own, [0]
    for masks in stages:
        parts = [blocks] + [send(blocks, axis, size, mask) for mask in masks[1:]]
        blocks = jnp.concatenate(parts[(len(offsets) == 1) :], axis=0)
        if len(offsets) == 1:
            blocks = blocks if len(stages) == 1 else jnp.concatenate([own, blocks], axis=0)
        offsets = [mask ^ offset for mask in masks for offset in offsets]
    if not stages:
        return [own, *early], list(last)
    rest = blocks if len(stages) == 1 else blocks[1:]
    late = [send(rest, axis, size, mask) for mask in last[1:]]
    pieces, order = [own, rest], list(offsets)
    for mask, own_piece, rest_piece in zip(last[1:], early, late, strict=True):
        pieces += [own_piece, rest_piece]
        order += [mask ^ offset for offset in offsets]
    return pieces, order


def pair_swap(part):
    return lax.ppermute(part, "head", [(0, 1), (1, 0)])


def params(held=0):
    return pltpu.CompilerParams(vmem_limit_bytes=(16 << 20) if held <= (16 << 20) else (60 << 20))


def row_column(shape, values):
    row = lax.broadcasted_iota(jnp.int32, shape, 0)
    out = jnp.zeros(shape, jnp.int32)
    for i, value in enumerate(values):
        out = jnp.where(row == i, value, out)
    return out


def bias_kernel(offsets, own_rows, keys, pos_ref, start_ref, bias_ref):
    queries = bias_ref.shape[0]
    me = lax.axis_index("ctx")
    places = [(me ^ int(off)) * own_rows + r for off in offsets for r in range(own_rows)]
    ids = me * keys + lax.broadcasted_iota(jnp.int32, (queries, keys), 1)
    first = row_column((queries, LANES), [start_ref[p] for p in places])[:, :1]
    last = row_column((queries, LANES), [pos_ref[p] for p in places])[:, :1]
    bias_ref[...] = jnp.where((ids >= first) & (ids <= last), 0.0, MASKED)


def fetch_kernel(*refs):
    count = (len(refs) - 1) // 2
    copies = [pltpu.make_async_copy(refs[i], refs[count + i], refs[-1].at[i]) for i in range(count)]
    for copy in copies:
        copy.start()
    for copy in copies:
        copy.wait()


def index_kernel(own_rows, heads, query_cols, key_ref, *refs):
    *piece_refs, rows_ref, gate_ref, part_ref, stack_ref = refs
    queries = rows_ref.shape[0]
    keys = key_ref.shape[0]
    at = 0
    for piece in piece_refs:
        for i in range(piece.shape[0]):
            rows_ref[at : at + own_rows, :] = piece[i]
            at += own_rows
    scale = (INDEX_DIM * INDEX_HEADS) ** (-0.5)
    weights = rows_ref[:, query_cols + heads * INDEX_DIM :].astype(f32) * scale
    for j in range(heads):
        col = query_cols + j * INDEX_DIM
        stack_ref[j * queries : (j + 1) * queries, :] = rows_ref[:, col : col + INDEX_DIM]
    chunk = 8
    total = jnp.zeros((queries, keys), f32)
    for c in range(0, heads, chunk):
        left = stack_ref[c * queries : (c + chunk) * queries, :]
        dotted = lax.dot_general(left, key_ref[...], (((1,), (1,)), ((), ())), preferred_element_type=f32)
        for j in range(chunk):
            one = dotted[j * queries : (j + 1) * queries]
            gate = jnp.where(one > 0, weights[:, c + j : c + j + 1], 0.0)
            gate_ref[c + j] = gate
            total = total + gate * one
    part_ref[...] = total


def score_kernel(rows_ref, w_ref, latent_ref, bias_ref, power_ref, peak_ref, lse_ref, *left_refs):
    queries = bias_ref.shape[0]
    heads, _, rank = w_ref.shape
    chunk = HEADS_A_STEP
    scale = WIDTH ** (-0.5)
    lane = lax.broadcasted_iota(jnp.int32, (queries, LANES), 1)

    def absorb(c, left_ref):
        for i in range(chunk):
            h = c * chunk + i
            own = rows_ref[:, h * WIDTH : (h + 1) * WIDTH]
            folded = jnp.dot(own[:, :NOPE_DIM], w_ref[h], preferred_element_type=f32)
            left_ref[i * queries : (i + 1) * queries, :rank] = folded.astype(bf16)
            left_ref[i * queries : (i + 1) * queries, rank:] = own[:, NOPE_DIM:]

    peaks = jnp.zeros((queries, LANES), f32)
    lses = jnp.zeros((queries, LANES), f32)
    absorb(0, left_refs[0])
    for c in range(heads // chunk):
        raw = jnp.dot(left_refs[c % len(left_refs)][...], latent_ref[...], preferred_element_type=f32)
        if c + 1 < heads // chunk:
            absorb(c + 1, left_refs[(c + 1) % len(left_refs)])
        for i in range(chunk):
            h = c * chunk + i
            one = raw[i * queries : (i + 1) * queries] + bias_ref[...]
            top = jnp.max(one, axis=1, keepdims=True)
            power = jnp.exp2((one - top) * (scale * LOG2E))
            power_ref[h] = power
            total = jnp.sum(power, axis=1, keepdims=True)
            peak = top * scale
            peaks = jnp.where(lane == h, peak, peaks)
            lses = jnp.where(lane == h, peak + jnp.log(total), lses)
    peak_ref[...] = peaks
    lse_ref[...] = lses


def packed_rows(heads, queries):
    a_row = LANES // heads
    return a_row, queries // a_row


def stats_kernel(offsets, own_rows, heads, part_ref, other_ref, bias_ref, lse_ref, send_ref, power_ref, peak_ref):
    queries = part_ref.shape[0]
    me = lax.axis_index("ctx")
    score = (part_ref[...] + other_ref[...]) + bias_ref[...]
    peak = jnp.max(score, axis=1, keepdims=True)
    power = jnp.exp(score - peak)
    power_ref[...] = power
    lse = peak + jnp.log(jnp.sum(power, axis=1, keepdims=True))
    lane = lax.broadcasted_iota(jnp.int32, (queries, LANES), 1)
    row = lax.broadcasted_iota(jnp.int32, (queries, LANES), 0)
    stats = jnp.where(lane == heads, lse, lse_ref[...])
    peak_ref[...] = jnp.broadcast_to(peak, (queries, LANES))
    place = {int(off): b for b, off in enumerate(offsets)}
    a_row, count = packed_rows(heads, queries)
    for away in range(len(offsets)):
        order = [place[away ^ int(off)] for off in offsets]
        moved = jnp.concatenate([stats[b * own_rows : (b + 1) * own_rows] for b in order], axis=0)
        packed = moved[:count]
        for i in range(1, a_row):
            packed = jnp.where(lane[:count] < i * heads, packed, pltpu.roll(moved[i * count : (i + 1) * count], i * heads, 1))
        line = jnp.sum(jnp.where(lane == row, moved[:, heads : heads + 1], 0.0), axis=0, keepdims=True)
        for i in range(count):
            send_ref[me ^ away, :, i * LANES : (i + 1) * LANES] = packed[i : i + 1]
        send_ref[me ^ away, :, count * LANES :] = line


def target_kernel(heads, every_ref, peak_ref, index_peak_ref, power_ref, index_power_ref, target_ref, predicted_ref):
    queries = peak_ref.shape[0]
    a_row, count = packed_rows(heads, queries)
    lines = []
    for i in range(count + 1):
        part = every_ref[:, 0, i * LANES : (i + 1) * LANES]
        top = jnp.max(part, axis=0, keepdims=True)
        lines.append(top + jnp.log(jnp.sum(jnp.exp(part - top), axis=0, keepdims=True)))
    packed = jnp.concatenate(lines[:count], axis=0)
    whole = jnp.concatenate([packed] + [pltpu.roll(packed, LANES - i * heads, 1) for i in range(1, a_row)], axis=0)
    lane = lax.broadcasted_iota(jnp.int32, (queries, LANES), 1)
    row = lax.broadcasted_iota(jnp.int32, (queries, LANES), 0)
    index_whole = jnp.sum(jnp.where(lane == row, lines[count], 0.0), axis=1, keepdims=True)
    factor = jnp.exp(peak_ref[...] - whole)
    predicted_ref[...] = index_power_ref[...] * jnp.exp(index_peak_ref[:, :1] - index_whole)
    total = power_ref[0] * factor[:, :1]
    for h in range(1, heads):
        total = total + power_ref[h] * factor[:, h : h + 1]
    target_ref[...] = total


def slope_kernel(offsets, own_rows, all_keys, predicted_ref, target_ref, other_ref, gate_ref, key_ref, slope_ref, send_ref):
    heads, queries, _ = gate_ref.shape
    me = lax.axis_index("ctx")
    target = (target_ref[...] + other_ref[...]) / MLA_HEADS
    misfit = (predicted_ref[...] - target) * all_keys
    chunk = 8
    for c in range(0, heads, chunk):
        slopes = jnp.concatenate([(misfit * gate_ref[c + j]).astype(bf16) for j in range(chunk)], axis=0)
        slope_ref[c * queries : (c + chunk) * queries, :] = slopes
        grad = jnp.dot(slopes, key_ref[...], preferred_element_type=f32).astype(send_ref.dtype)
        for j in range(chunk):
            col = (c + j) * INDEX_DIM
            for b, off in enumerate(offsets):
                at = j * queries + b * own_rows
                send_ref[me ^ int(off), :, col : col + INDEX_DIM] = grad[at : at + own_rows]


def shards(q_heads, w_uk, latent_t, index_query, index_key, head_weight, query_pos, key_start):
    own_rows = q_heads.shape[0]
    ctx = lax.axis_size("ctx")
    latent_dim, keys = latent_t.shape
    local_heads, _, _ = w_uk.shape
    index_local = head_weight.shape[1]
    queries = own_rows * ctx
    shape = jax.ShapeDtypeStruct

    pad = jnp.zeros((own_rows, -index_local % LANES), bf16)
    own = jnp.concatenate([q_heads, index_query, head_weight, pad], axis=1)
    pieces, offsets = gather_pieces(own[None], "ctx", ctx)

    bias = pl.pallas_call(
        functools.partial(bias_kernel, offsets, own_rows, keys),
        out_shape=shape((queries, keys), f32),
        in_specs=[SMEM_WHOLE] * 2,
        out_specs=VMEM_WHOLE,
        compiler_params=params(),
        name="bias",
    )(query_pos, key_start)
    held = (w_uk, latent_t, index_key)
    w_uk, latent_t, index_key = pl.pallas_call(
        fetch_kernel,
        out_shape=tuple(shape(a.shape, a.dtype) for a in held),
        in_specs=[HBM_WHOLE] * len(held),
        out_specs=(VMEM_WHOLE,) * len(held),
        scratch_shapes=[pltpu.SemaphoreType.DMA((len(held),))],
        compiler_params=params(),
        name="fetch",
    )(*held)

    rows, gate, part, stack = pl.pallas_call(
        functools.partial(index_kernel, own_rows, index_local, q_heads.shape[1]),
        out_shape=(
            shape((queries, own.shape[1]), bf16),
            shape((index_local, queries, keys), f32),
            shape((queries, keys), f32),
            shape((index_local * queries, INDEX_DIM), bf16),
        ),
        in_specs=[VMEM_WHOLE] * (1 + len(pieces)),
        out_specs=(VMEM_WHOLE,) * 4,
        compiler_params=params(4 * index_local * queries * keys),
        name="index",
    )(index_key, *pieces)
    other_part = pair_swap(part)

    powers, peaks, lses = pl.pallas_call(
        score_kernel,
        out_shape=(
            shape((local_heads, queries, keys), f32),
            shape((queries, LANES), f32),
            shape((queries, LANES), f32),
        ),
        in_specs=[VMEM_WHOLE] * 4,
        out_specs=(VMEM_WHOLE,) * 3,
        scratch_shapes=[pltpu.VMEM((HEADS_A_STEP * queries, latent_dim), bf16)] * 3,
        compiler_params=params(4 * local_heads * queries * keys),
        name="scores",
    )(rows, w_uk, latent_t, bias)

    send, index_powers, index_peaks = pl.pallas_call(
        functools.partial(stats_kernel, offsets, own_rows, local_heads),
        out_shape=(
            shape((ctx, 1, (packed_rows(local_heads, queries)[1] + 1) * LANES), f32),
            shape((queries, keys), f32),
            shape((queries, LANES), f32),
        ),
        in_specs=[VMEM_WHOLE] * 4,
        out_specs=(VMEM_WHOLE,) * 3,
        compiler_params=params(),
        name="stats",
    )(part, other_part, bias, lses)
    every = lax.all_to_all(send, "ctx", 0, 0, tiled=True)

    target, predicted = pl.pallas_call(
        functools.partial(target_kernel, local_heads),
        out_shape=(shape((queries, keys), f32), shape((queries, keys), f32)),
        in_specs=[VMEM_WHOLE] * 5,
        out_specs=(VMEM_WHOLE,) * 2,
        compiler_params=params(4 * local_heads * queries * keys),
        name="target",
    )(every, peaks, index_peaks, powers, index_powers)
    other_target = pair_swap(target)

    slopes, to_owner = pl.pallas_call(
        functools.partial(slope_kernel, offsets, own_rows, keys * ctx),
        out_shape=(
            shape((index_local * queries, keys), bf16),
            shape((ctx, own_rows, index_local * INDEX_DIM), bf16),
        ),
        in_specs=[VMEM_WHOLE] * 5,
        out_specs=(VMEM_WHOLE,) * 2,
        compiler_params=params(4 * index_local * queries * keys),
        name="slopes",
    )(predicted, target, other_target, gate, index_key)
    grad_query = jnp.sum(lax.all_to_all(to_owner, "ctx", 0, 0, tiled=True).astype(f32), axis=0)

    grad_key_part = lax.dot_general(slopes, stack, (((0,), (0,)), ((), ())), preferred_element_type=f32)
    grad_key = grad_key_part + pair_swap(grad_key_part)
    along = (grad_query * index_query.astype(f32)).reshape(own_rows, index_local, INDEX_DIM)
    grad_weight = jnp.sum(along, axis=2) / head_weight.astype(f32)
    return grad_query, grad_key, grad_weight


def solution(mesh):
    placed = (
        P("ctx", "head"),
        P("head", None, None),
        P(None, "ctx"),
        P("ctx", "head"),
        P("ctx", None),
        P("ctx", "head"),
        P(),
        P(),
    )
    return jax.shard_map(
        shards,
        mesh=mesh,
        in_specs=placed,
        out_specs=(P("ctx", "head"), P("ctx", None), P("ctx", "head")),
        check_vma=False,
    )
```

profile of v0, /device:TPU:0, one launch (start us, length us, event | category | flops | bytes accessed | tf_op | source)
XLA Modules:
  0.0 75.5 jit_solution(12161622569130543570)
XLA Ops:
  0.6 1.0 %concatenate.6 = bf16[2,16512]{1,0:T(2,128)(2,1)S(1)} concatenate(bf16[2,12288]{1,0:T(2,128)(2,1)} %param.8, bf16[2,4096]{1,0:T(2,128)(2,1)} %param.11, bf16[2,32]{1,0:T(2,128)(2,1)} %param.13, bf16[2,96]{1,0:T(2,128)(2,1)S(1)} %broadcast_in_dim.6), dimensions={1} | concatenate | bytes 132096 | tf_op jit(solution)/shard_map/concatenate | solution.py:243
  1.6 3.1 %collective-permute-start = (bf16[1,2,16512]{2,1,0:T(2,128)(2,1)S(1)}, bf16[1,2,16512]{2,1,0:T(2,128)(2,1)S(1)}, u32[]{:S(2)}, u32[]{:S(2)}) collective-permute-start(bf16[1,2,16512]{2,1,0:T(2,128)(2,1)S(1)} %bitcast.7), channel_id=1, source_target_pairs={{0,8},{2,10},{4,12},{6,14},{8,0},{10,2},{12,4},{14,6},{16,24},{18,... | collective-permute-start | bytes 198152 | tf_op jit(solution)/shard_map/ppermute | solution.py:42
  4.7 2.5 %collective-permute-start.2 = (bf16[1,2,16512]{2,1,0:T(2,128)(2,1)S(1)}, bf16[1,2,16512]{2,1,0:T(2,128)(2,1)S(1)}, u32[]{:S(2)}, u32[]{:S(2)}) collective-permute-start(bf16[1,2,16512]{2,1,0:T(2,128)(2,1)S(1)} %bitcast.8), channel_id=1, source_target_pairs={{0,24},{2,26},{4,28},{6,30},{8,16},{10,18},{12,20},{14,22},{16,8},... | collective-permute-start | bytes 198152 | tf_op jit(solution)/shard_map/ppermute | solution.py:42
  7.2 0.1 collective-permute-start.1
  7.3 0.0 collective-permute-done
  7.4 6.3 %collective-permute-done.1 = bf16[1,2,16512]{2,1,0:T(2,128)(2,1)S(1)} collective-permute-done((bf16[1,2,16512]{2,1,0:T(2,128)(2,1)S(1)}, bf16[1,2,16512]{2,1,0:T(2,128)(2,1)S(1)}, u32[]{:S(2)}, u32[]{:S(2)}) %collective-permute-start.1) | collective-permute-done | bytes 66080 | tf_op jit(solution)/shard_map/ppermute | solution.py:42
  13.7 0.1 constant_dynamic-update-slice_fusion.1
  13.7 0.0 collective-permute-done.2
  13.7 0.0 copy-start.3
  13.8 0.0 copy-start.4
  13.8 0.1 constant_dynamic-update-slice_fusion.refs_1_
  13.8 2.5 %collective-permute-start.8 = (bf16[3,2,16512]{2,1,0:T(2,128)(2,1)S(1)}, bf16[3,2,16512]{2,1,0:T(2,128)(2,1)S(1)}, u32[]{:S(2)}, u32[]{:S(2)}) collective-permute-start(bf16[3,2,16512]{2,1,0:T(2,128)(2,1)S(1)} %constant_dynamic-update-slice_fusion.refs_1_), channel_id=1, source_target_pairs={{0,6},{2,4},{4,2},{6,0},{8,14},{10,12},{12,10},{14,8},{16,22},{18,... | collective-permute-start | bytes 594440 | tf_op jit(solution)/shard_map/ppermute | solution.py:42
  16.3 0.5 collective-permute-start.6
  16.9 0.5 collective-permute-start.4
  17.4 2.4 %collective-permute-start.7 = (bf16[1,2,16512]{2,1,0:T(2,128)(2,1)S(1)}, bf16[1,2,16512]{2,1,0:T(2,128)(2,1)S(1)}, u32[]{:S(2)}, u32[]{:S(2)}) collective-permute-start(bf16[1,2,16512]{2,1,0:T(2,128)(2,1)S(1)} %bitcast.10), channel_id=1, source_target_pairs={{0,6},{2,4},{4,2},{6,0},{8,14},{10,12},{12,10},{14,8},{16,22},{18,... | collective-permute-start | bytes 198152 | tf_op jit(solution)/shard_map/ppermute | solution.py:42
  19.8 0.5 collective-permute-start.5
  20.3 7.1 %collective-permute-done.7.refs_6_ = bf16[1,2,16512]{2,1,0:T(2,128)(2,1)S(1)} collective-permute-done((bf16[1,2,16512]{2,1,0:T(2,128)(2,1)S(1)}, bf16[1,2,16512]{2,1,0:T(2,128)(2,1)S(1)}, u32[]{:S(2)}, u32[]{:S(2)}) %collective-permute-start.7) | collective-permute-done | bytes 66080 | tf_op jit(solution)/shard_map/ppermute | solution.py:42
  27.4 1.5 %collective-permute-start.3 = (bf16[1,2,16512]{2,1,0:T(2,128)(2,1)S(1)}, bf16[1,2,16512]{2,1,0:T(2,128)(2,1)S(1)}, u32[]{:S(2)}, u32[]{:S(2)}) collective-permute-start(bf16[1,2,16512]{2,1,0:T(2,128)(2,1)S(1)} %bitcast.12), channel_id=1, source_target_pairs={{0,2},{2,0},{4,6},{6,4},{8,10},{10,8},{12,14},{14,12},{16,18},{18,... | collective-permute-start | bytes 198152 | tf_op jit(solution)/shard_map/ppermute | solution.py:42
  28.9 3.4 %copy-done = bf16[64,128,512]{2,1,0:T(8,128)(2,1)S(1)} copy-done((bf16[64,128,512]{2,1,0:T(8,128)(2,1)S(1)}, bf16[64,128,512]{2,1,0:T(8,128)(2,1)}, u32[]{:S(2)}) %copy-start) | copy-done | bytes 8388632
  32.3 1.3 %copy-done.1 = bf16[576,1024]{1,0:T(8,128)(2,1)S(1)} copy-done((bf16[576,1024]{1,0:T(8,128)(2,1)S(1)}, bf16[576,1024]{1,0:T(8,128)(2,1)}, u32[]{:S(2)}) %copy-start.1) | copy-done | bytes 1179672
  33.6 0.9 %copy-done.2 = bf16[1024,128]{1,0:T(8,128)(2,1)S(1)} copy-done((bf16[1024,128]{1,0:T(8,128)(2,1)S(1)}, bf16[1024,128]{1,0:T(8,128)(2,1)}, u32[]{:S(2)}) %copy-start.2) | copy-done | bytes 262168
  34.5 0.8 %fetch.1 = (bf16[64,128,512]{2,1,0:T(8,128)(2,1)S(1)}, bf16[576,1024]{1,0:T(8,128)(2,1)S(1)}, bf16[1024,128]{1,0:T(8,128)(2,1)S(1)}) custom-call(bf16[64,128,512]{2,1,0:T(8,128)(2,1)S(1)} %copy-done, bf16[576,1024]{1,0:T(8,128)(2,1)S(1)} %copy-done.1, bf16[1024,128]{1,0:T(8,128)(2,1)S(1)} %copy-done.2), custom_call_target="tpu_custom_call" | custom-call | tf_op jit(solution)/shard_map/fetch/pallas_call | solution.py:255
  35.4 0.0 collective-permute-done.5.refs_4_
  35.4 0.0 collective-permute-done.3.refs_2_
  35.4 0.0 collective-permute-done.6.refs_5_
  35.4 0.0 collective-permute-done.4.refs_3_
  35.4 1.3 %index.1 = (bf16[32,16512]{1,0:T(8,128)(2,1)S(1)}, f32[32,32,1024]{2,1,0:T(8,128)S(1)}, f32[32,1024]{1,0:T(8,128)S(1)}, bf16[1024,128]{1,0:T(8,128)(2,1)S(1)}) custom-call(bf16[1024,128]{1,0:T(8,128)(2,1)S(1)} %get-tuple-element.20.key_ref, bf16[1,2,16512]{2,1,0:T(2,128)(2,1)S(1)} %bitcast.13, ...), custom_call_target="tpu_custom_call" | custom-call | tf_op jit(solution)/shard_map/index/pallas_call | solution.py:265
  36.8 0.1 collective-permute-start.9
  36.9 0.6 bias.1.bias_ref
  37.5 6.0 %scores.1 = (f32[64,32,1024]{2,1,0:T(8,128)S(1)}, f32[32,128]{1,0:T(8,128)S(1)}, f32[32,128]{1,0:T(8,128)S(1)}) custom-call(bf16[32,16512]{1,0:T(8,128)(2,1)S(1)} %get-tuple-element.22.rows_ref, bf16[64,128,512]{2,1,0:T(8,128)(2,1)S(1)} %get-tuple-element.23.w_ref, bf16[576,1024]{1,0:T(8,128)(2,1)S(1)} %get-tuple-element.24.latent_ref, ...), custom_call_target="tpu_custom_call" | custom-call | tf_op jit(solution)/shard_map/scores/pallas_call | solution.py:280
  43.5 0.0 collective-permute-done.9.other_ref
  43.5 0.4 stats.1
  43.9 11.8 %all_to_all.10.every_ref = f32[16,1,2176]{2,1,0:T(1,128)S(1)} all-to-all(f32[16,1,2176]{2,1,0:T(1,128)S(1)} %get-tuple-element.26), channel_id=1, replica_groups=mesh['ctx'=16,'head'=2] {'ctx'}, dimensions={0} | all-to-all | bytes 278528 | tf_op jit(solution)/shard_map/all_to_all | solution.py:306
  55.7 1.0 %target.1 = (f32[32,1024]{1,0:T(8,128)S(1)}, f32[32,1024]{1,0:T(8,128)S(1)}) custom-call(f32[16,1,2176]{2,1,0:T(1,128)S(1)} %all_to_all.10.every_ref, f32[32,128]{1,0:T(8,128)S(1)} %get-tuple-element.27.peak_ref, f32[32,128]{1,0:T(8,128)S(1)} %get-tuple-element.28.index_peak_ref, f32[64,32,1024]{2,1,0:T(8,128)S(1)} %get-tuple-element.29.power_ref, ...), custom_call_target="tpu_custom_call" | custom-call | tf_op jit(solution)/shard_map/target/pallas_call | solution.py:308
  56.7 0.1 collective-permute-start.10
  56.8 1.3 %collective-permute-done.10.other_ref = f32[32,1024]{1,0:T(8,128)S(1)} collective-permute-done((f32[32,1024]{1,0:T(8,128)S(1)}, f32[32,1024]{1,0:T(8,128)S(1)}, u32[]{:S(2)}, u32[]{:S(2)}) %collective-permute-start.10) | collective-permute-done | bytes 131104 | tf_op jit(solution)/shard_map/ppermute | solution.py:67
  58.1 1.6 %slopes.1 = (bf16[1024,1024]{1,0:T(8,128)(2,1)S(1)}, bf16[16,2,4096]{2,1,0:T(2,128)(2,1)}) custom-call(f32[32,1024]{1,0:T(8,128)S(1)} %get-tuple-element.31.predicted_ref, f32[32,1024]{1,0:T(8,128)S(1)} %get-tuple-element.32.target_ref, f32[32,1024]{1,0:T(8,128)S(1)} %collective-permute-done.10.other_ref, f32[32,32,1024]{2,1,0:T(8,128)S(1)} %get-tuple-element.33.gate_ref, ...), custom_call_target="tpu_custom_call" | custom-call | tf_op jit(solution)/shard_map/slopes/pallas_call | solution.py:318
  59.7 3.5 %all-to-all-start.1 = ((bf16[16,2,4096]{2,1,0:T(2,128)(2,1)}), bf16[16,2,4096]{2,1,0:T(2,128)(2,1)S(1)}, u32[]{:S(2)}, u32[]{:S(2)}) async-start(bf16[16,2,4096]{2,1,0:T(2,128)(2,1)} %get-tuple-element.34), calls=%async_computation.1 | async-start | bytes 524288 | tf_op jit(solution)/shard_map/all_to_all | solution.py:329
  63.3 0.0 copy-start.6
  63.3 0.0 copy-start.7
  63.3 0.7 fusion
  64.0 0.2 collective-permute-start.11
  64.2 9.4 %all-to-all-done.1 = bf16[16,2,4096]{2,1,0:T(2,128)(2,1)S(1)} async-done(((bf16[16,2,4096]{2,1,0:T(2,128)(2,1)}), bf16[16,2,4096]{2,1,0:T(2,128)(2,1)S(1)}, u32[]{:S(2)}, u32[]{:S(2)}) %all-to-all-start.1) | async-done | bytes 262176 | tf_op jit(solution)/shard_map/all_to_all | solution.py:329
  73.7 0.2 convert_reduce_fusion
  73.9 0.0 copy-start.5
  73.9 0.1 bitcast_reduce_fusion
  74.0 0.6 convert_divide_fusion
  74.6 0.8 %add.3 = f32[1024,128]{1,0:T(8,128)} add(f32[1024,128]{1,0:T(8,128)S(1)} %fusion, f32[1024,128]{1,0:T(8,128)S(1)} %collective-permute-done.11) | non-fusion elementwise | flops 131072 | bytes 1572864 | tf_op jit(solution)/shard_map/add | solution.py:332
  (13 shorter events, 0.1 us)
Async XLA Ops:
  1.6 5.7 %collective-permute-start = (bf16[1,2,16512]{2,1,0:T(2,128)(2,1)S(1)}, bf16[1,2,16512]{2,1,0:T(2,128)(2,1)S(1)}, u32[]{:S(2)}, u32[]{:S(2)}) collective-permute-start(bf16[1,2,16512]{2,1,0:T(2,128)(2,1)S(1)} %bitcast.7), channel_id=1, source_target_pairs={{0,8},{2,10},{4,12},{6,14},{8,0},{10,2},{12,4},{14,6},{16,24},{18,... | collective-permute-start | bytes 198152 | tf_op jit(solution)/shard_map/ppermute | solution.py:42
  4.7 9.0 %collective-permute-start.2 = (bf16[1,2,16512]{2,1,0:T(2,128)(2,1)S(1)}, bf16[1,2,16512]{2,1,0:T(2,128)(2,1)S(1)}, u32[]{:S(2)}, u32[]{:S(2)}) collective-permute-start(bf16[1,2,16512]{2,1,0:T(2,128)(2,1)S(1)} %bitcast.8), channel_id=1, source_target_pairs={{0,24},{2,26},{4,28},{6,30},{8,16},{10,18},{12,20},{14,22},{16,8},... | collective-permute-start | bytes 198152 | tf_op jit(solution)/shard_map/ppermute | solution.py:42
  7.2 6.5 %collective-permute-start.1 = (bf16[1,2,16512]{2,1,0:T(2,128)(2,1)S(1)}, bf16[1,2,16512]{2,1,0:T(2,128)(2,1)S(1)}, u32[]{:S(2)}, u32[]{:S(2)}) collective-permute-start(bf16[1,2,16512]{2,1,0:T(2,128)(2,1)S(1)} %bitcast.9), channel_id=1, source_target_pairs={{0,16},{2,18},{4,20},{6,22},{8,24},{10,26},{12,28},{14,30},{16,0},... | collective-permute-start | bytes 198152 | tf_op jit(solution)/shard_map/ppermute | solution.py:42
  13.7 23.1 %copy-start.3 = (s32[32]{0:T(128)S(1)}, s32[32]{0:T(128)}, u32[]{:S(2)}) copy-start(s32[32]{0:T(128)} %pos_ref.1) | copy-start | bytes 388
  13.8 23.1 %copy-start.4 = (s32[32]{0:T(128)S(1)}, s32[32]{0:T(128)}, u32[]{:S(2)}) copy-start(s32[32]{0:T(128)} %start_ref.1) | copy-start | bytes 388
  13.8 21.5 %collective-permute-start.8 = (bf16[3,2,16512]{2,1,0:T(2,128)(2,1)S(1)}, bf16[3,2,16512]{2,1,0:T(2,128)(2,1)S(1)}, u32[]{:S(2)}, u32[]{:S(2)}) collective-permute-start(bf16[3,2,16512]{2,1,0:T(2,128)(2,1)S(1)} %constant_dynamic-update-slice_fusion.refs_1_), channel_id=1, source_target_pairs={{0,6},{2,4},{4,2},{6,0},{8,14},{10,12},{12,10},{14,8},{16,22},{18,... | collective-permute-start | bytes 594440 | tf_op jit(solution)/shard_map/ppermute | solution.py:42
  16.3 19.0 %collective-permute-start.6 = (bf16[3,2,16512]{2,1,0:T(2,128)(2,1)S(1)}, bf16[3,2,16512]{2,1,0:T(2,128)(2,1)S(1)}, u32[]{:S(2)}, u32[]{:S(2)}) collective-permute-start(bf16[3,2,16512]{2,1,0:T(2,128)(2,1)S(1)} %constant_dynamic-update-slice_fusion.refs_1_), channel_id=1, source_target_pairs={{0,4},{2,6},{4,0},{6,2},{8,12},{10,14},{12,8},{14,10},{16,20},{18,... | collective-permute-start | bytes 594440 | tf_op jit(solution)/shard_map/ppermute | solution.py:42
  16.9 18.5 %collective-permute-start.4 = (bf16[3,2,16512]{2,1,0:T(2,128)(2,1)S(1)}, bf16[3,2,16512]{2,1,0:T(2,128)(2,1)S(1)}, u32[]{:S(2)}, u32[]{:S(2)}) collective-permute-start(bf16[3,2,16512]{2,1,0:T(2,128)(2,1)S(1)} %constant_dynamic-update-slice_fusion.refs_1_), channel_id=1, source_target_pairs={{0,2},{2,0},{4,6},{6,4},{8,10},{10,8},{12,14},{14,12},{16,18},{18,... | collective-permute-start | bytes 594440 | tf_op jit(solution)/shard_map/ppermute | solution.py:42
  17.4 10.0 %collective-permute-start.7 = (bf16[1,2,16512]{2,1,0:T(2,128)(2,1)S(1)}, bf16[1,2,16512]{2,1,0:T(2,128)(2,1)S(1)}, u32[]{:S(2)}, u32[]{:S(2)}) collective-permute-start(bf16[1,2,16512]{2,1,0:T(2,128)(2,1)S(1)} %bitcast.10), channel_id=1, source_target_pairs={{0,6},{2,4},{4,2},{6,0},{8,14},{10,12},{12,10},{14,8},{16,22},{18,... | collective-permute-start | bytes 198152 | tf_op jit(solution)/shard_map/ppermute | solution.py:42
  19.8 15.5 %collective-permute-start.5 = (bf16[1,2,16512]{2,1,0:T(2,128)(2,1)S(1)}, bf16[1,2,16512]{2,1,0:T(2,128)(2,1)S(1)}, u32[]{:S(2)}, u32[]{:S(2)}) collective-permute-start(bf16[1,2,16512]{2,1,0:T(2,128)(2,1)S(1)} %bitcast.11), channel_id=1, source_target_pairs={{0,4},{2,6},{4,0},{6,2},{8,12},{10,14},{12,8},{14,10},{16,20},{18,... | collective-permute-start | bytes 198152 | tf_op jit(solution)/shard_map/ppermute | solution.py:42
  27.4 8.0 %collective-permute-start.3 = (bf16[1,2,16512]{2,1,0:T(2,128)(2,1)S(1)}, bf16[1,2,16512]{2,1,0:T(2,128)(2,1)S(1)}, u32[]{:S(2)}, u32[]{:S(2)}) collective-permute-start(bf16[1,2,16512]{2,1,0:T(2,128)(2,1)S(1)} %bitcast.12), channel_id=1, source_target_pairs={{0,2},{2,0},{4,6},{6,4},{8,10},{10,8},{12,14},{14,12},{16,18},{18,... | collective-permute-start | bytes 198152 | tf_op jit(solution)/shard_map/ppermute | solution.py:42
  28.9 3.4 %copy-start = (bf16[64,128,512]{2,1,0:T(8,128)(2,1)S(1)}, bf16[64,128,512]{2,1,0:T(8,128)(2,1)}, u32[]{:S(2)}) copy-start(bf16[64,128,512]{2,1,0:T(8,128)(2,1)} %refs_0_.1) | copy-start | bytes 25165828
  32.3 1.3 %copy-start.1 = (bf16[576,1024]{1,0:T(8,128)(2,1)S(1)}, bf16[576,1024]{1,0:T(8,128)(2,1)}, u32[]{:S(2)}) copy-start(bf16[576,1024]{1,0:T(8,128)(2,1)} %refs_1_.1) | copy-start | bytes 3538948
  33.5 0.9 %copy-start.2 = (bf16[1024,128]{1,0:T(8,128)(2,1)S(1)}, bf16[1024,128]{1,0:T(8,128)(2,1)}, u32[]{:S(2)}) copy-start(bf16[1024,128]{1,0:T(8,128)(2,1)} %refs_2_.1) | copy-start | bytes 786436
  36.8 6.7 %collective-permute-start.9 = (f32[32,1024]{1,0:T(8,128)S(1)}, f32[32,1024]{1,0:T(8,128)S(1)}, u32[]{:S(2)}, u32[]{:S(2)}) collective-permute-start(f32[32,1024]{1,0:T(8,128)S(1)} %get-tuple-element.21.part_ref), channel_id=1, source_target_pairs={{0,1},{1,0},{2,3},{3,2},{4,5},{5,4},{6,7},{7,6},{8,9},{9,8},{10,11... | collective-permute-start | bytes 393224 | tf_op jit(solution)/shard_map/ppermute | solution.py:67
  56.7 1.4 %collective-permute-start.10 = (f32[32,1024]{1,0:T(8,128)S(1)}, f32[32,1024]{1,0:T(8,128)S(1)}, u32[]{:S(2)}, u32[]{:S(2)}) collective-permute-start(f32[32,1024]{1,0:T(8,128)S(1)} %get-tuple-element.32.target_ref), channel_id=1, source_target_pairs={{0,1},{1,0},{2,3},{3,2},{4,5},{5,4},{6,7},{7,6},{8,9},{9,8},{10,11... | collective-permute-start | bytes 393224 | tf_op jit(solution)/shard_map/ppermute | solution.py:67
  59.7 13.9 %all-to-all-start.1 = ((bf16[16,2,4096]{2,1,0:T(2,128)(2,1)}), bf16[16,2,4096]{2,1,0:T(2,128)(2,1)S(1)}, u32[]{:S(2)}, u32[]{:S(2)}) async-start(bf16[16,2,4096]{2,1,0:T(2,128)(2,1)} %get-tuple-element.34), calls=%async_computation.1 | async-start | bytes 524288 | tf_op jit(solution)/shard_map/all_to_all | solution.py:329
  63.3 10.6 %copy-start.6 = (bf16[2,4096]{1,0:T(2,128)(2,1)S(1)}, bf16[2,4096]{1,0:T(2,128)(2,1)}, u32[]{:S(2)}) copy-start(bf16[2,4096]{1,0:T(2,128)(2,1)} %param.11) | copy-start | bytes 49156
  63.3 10.7 %copy-start.7 = (bf16[2,32]{1,0:T(2,128)(2,1)S(1)}, bf16[2,32]{1,0:T(2,128)(2,1)}, u32[]{:S(2)}) copy-start(bf16[2,32]{1,0:T(2,128)(2,1)} %param.13) | copy-start | bytes 388
  64.0 10.6 %collective-permute-start.11 = (f32[1024,128]{1,0:T(8,128)S(1)}, f32[1024,128]{1,0:T(8,128)S(1)}, u32[]{:S(2)}, u32[]{:S(2)}) collective-permute-start(f32[1024,128]{1,0:T(8,128)S(1)} %fusion), channel_id=1, source_target_pairs={{0,1},{1,0},{2,3},{3,2},{4,5},{5,4},{6,7},{7,6},{8,9},{9,8},{10,11... | collective-permute-start | bytes 1572872 | tf_op jit(solution)/shard_map/ppermute | solution.py:67
  73.9 1.6 %copy-start.5 = (f32[2,4096]{1,0:T(2,128)}, f32[2,4096]{1,0:T(2,128)S(1)}, u32[]{:S(2)}) copy-start(f32[2,4096]{1,0:T(2,128)S(1)} %convert_reduce_fusion) | copy-start | bytes 98308
where the time goes:
time: 75.9 us; the launch traced here: 75.5 us
  waiting for transfers between devices  24.2 us (32%)
  starting transfers between devices  17.6 us (23%)
  Pallas kernels  11.8 us (16%)
  blocking collectives  11.8 us (16%)
  local copies, waits for them, and re-layouts  6.79 us (9%)
  other arithmetic  1.75 us (2%)
  between operations  0.85 us (1%)
    ppermute x9, starting transfers between devices, send(): return lax.ppermute(block, axis, [(i, i ^ mask) for i in range(size)])  13.7 us
    ppermute x9, waiting for transfers between devices, send(): return lax.ppermute(block, axis, [(i, i ^ mask) for i in range(size)])  13.4 us
    all_to_all x1, blocking collectives, shards(): every = lax.all_to_all(send, 'ctx', 0, 0, tiled=True)  11.8 us
    all_to_all x1, waiting for transfers between devices, shards(): lax.all_to_all(to_owner, 'ctx', 0, 0, tiled=True).astype(f32)  9.43 us
    pallas_call x1, Pallas kernels, shards(): pl.pallas_call(score_kernel, out_shape=(shape((local_heads, queries, keys...  5.98 us
    unnamed x18, local copies, waits for them, and re-layouts  5.74 us
    all_to_all x1, starting transfers between devices, shards(): lax.all_to_all(to_owner, 'ctx', 0, 0, tiled=True).astype(f32)  3.53 us
    pallas_call x1, Pallas kernels, shards(): pl.pallas_call(functools.partial(slope_kernel, offsets, own_rows, keys *...  1.64 us
  transfers between devices with their start and end apart: 13, of which 4 were waited for; matrix products, arithmetic and copies ran while one was open for 2% of the time, Pallas kernels for 10%

commit v1 on v0

--- a/solution.py
+++ b/solution.py
@@ -326,10 +326,12 @@
         compiler_params=params(4 * index_local * queries * keys),
         name="slopes",
     )(predicted, target, other_target, gate, index_key)
-    grad_query = jnp.sum(lax.all_to_all(to_owner, "ctx", 0, 0, tiled=True).astype(f32), axis=0)
+    from_all = lax.all_to_all(to_owner, "ctx", 0, 0, tiled=True)
+    grad_query = jnp.sum(from_all.astype(f32), axis=0)
 
     grad_key_part = lax.dot_general(slopes, stack, (((0,), (0,)), ((), ())), preferred_element_type=f32)
-    grad_key = grad_key_part + pair_swap(grad_key_part)
+    other_key = pair_swap(grad_key_part)
+    grad_key = grad_key_part + other_key
     along = (grad_query * index_query.astype(f32)).reshape(own_rows, index_local, INDEX_DIM)
     grad_weight = jnp.sum(along, axis=2) / head_weight.astype(f32)
     return grad_query, grad_key, grad_weight

time: 75.9 us -> 75.9 us (level)
  no operation moved by 1% of the time
where the time goes in v1:
time: 75.9 us; the launch traced here: 75.5 us
  waiting for transfers between devices  24.2 us (32%)
  starting transfers between devices  17.6 us (23%)
  Pallas kernels  11.8 us (16%)
  blocking collectives  11.8 us (16%)
  local copies, waits for them, and re-layouts  6.79 us (9%)
  other arithmetic  1.75 us (2%)
  between operations  0.85 us (1%)
    ppermute x9, starting transfers between devices, send(): return lax.ppermute(block, axis, [(i, i ^ mask) for i in range(size)])  13.7 us
    ppermute x9, waiting for transfers between devices, send(): return lax.ppermute(block, axis, [(i, i ^ mask) for i in range(size)])  13.4 us
    all_to_all x1, blocking collectives, shards(): every = lax.all_to_all(send, 'ctx', 0, 0, tiled=True)  11.8 us
    all_to_all x1, waiting for transfers between devices, shards(): from_all = lax.all_to_all(to_owner, 'ctx', 0, 0, tiled=True)  9.43 us
    pallas_call x1, Pallas kernels, shards(): pl.pallas_call(score_kernel, out_shape=(shape((local_heads, queries, keys...  5.98 us
    unnamed x18, local copies, waits for them, and re-layouts  5.74 us
    all_to_all x1, starting transfers between devices, shards(): from_all = lax.all_to_all(to_owner, 'ctx', 0, 0, tiled=True)  3.53 us
    pallas_call x1, Pallas kernels, shards(): pl.pallas_call(functools.partial(slope_kernel, offsets, own_rows, keys *...  1.64 us
  transfers between devices with their start and end apart: 13, of which 4 were waited for; matrix products, arithmetic and copies ran while one was open for 2% of the time, Pallas kernels for 10%

profile of v1, /device:TPU:0, one launch (start us, length us, event | category | flops | bytes accessed | tf_op | source)
XLA Modules:
  0.0 75.5 jit_solution(12161622569130543570)
XLA Ops:
  0.6 1.0 %concatenate.6 = bf16[2,16512]{1,0:T(2,128)(2,1)S(1)} concatenate(bf16[2,12288]{1,0:T(2,128)(2,1)} %param.8, bf16[2,4096]{1,0:T(2,128)(2,1)} %param.11, bf16[2,32]{1,0:T(2,128)(2,1)} %param.13, bf16[2,96]{1,0:T(2,128)(2,1)S(1)} %broadcast_in_dim.6), dimensions={1} | concatenate | bytes 132096 | tf_op jit(solution)/shard_map/concatenate | solution.py:243
  1.6 3.1 %collective-permute-start = (bf16[1,2,16512]{2,1,0:T(2,128)(2,1)S(1)}, bf16[1,2,16512]{2,1,0:T(2,128)(2,1)S(1)}, u32[]{:S(2)}, u32[]{:S(2)}) collective-permute-start(bf16[1,2,16512]{2,1,0:T(2,128)(2,1)S(1)} %bitcast.7), channel_id=1, source_target_pairs={{0,8},{2,10},{4,12},{6,14},{8,0},{10,2},{12,4},{14,6},{16,24},{18,... | collective-permute-start | bytes 198152 | tf_op jit(solution)/shard_map/ppermute | solution.py:42
  4.7 2.5 %collective-permute-start.2 = (bf16[1,2,16512]{2,1,0:T(2,128)(2,1)S(1)}, bf16[1,2,16512]{2,1,0:T(2,128)(2,1)S(1)}, u32[]{:S(2)}, u32[]{:S(2)}) collective-permute-start(bf16[1,2,16512]{2,1,0:T(2,128)(2,1)S(1)} %bitcast.8), channel_id=1, source_target_pairs={{0,24},{2,26},{4,28},{6,30},{8,16},{10,18},{12,20},{14,22},{16,8},... | collective-permute-start | bytes 198152 | tf_op jit(solution)/shard_map/ppermute | solution.py:42
  7.2 0.1 collective-permute-start.1
  7.3 0.0 collective-permute-done
  7.4 6.3 %collective-permute-done.1 = bf16[1,2,16512]{2,1,0:T(2,128)(2,1)S(1)} collective-permute-done((bf16[1,2,16512]{2,1,0:T(2,128)(2,1)S(1)}, bf16[1,2,16512]{2,1,0:T(2,128)(2,1)S(1)}, u32[]{:S(2)}, u32[]{:S(2)}) %collective-permute-start.1) | collective-permute-done | bytes 66080 | tf_op jit(solution)/shard_map/ppermute | solution.py:42
  13.7 0.1 constant_dynamic-update-slice_fusion.1
  13.7 0.0 collective-permute-done.2
  13.7 0.0 copy-start.3
  13.8 0.0 copy-start.4
  13.8 0.1 constant_dynamic-update-slice_fusion.refs_1_
  13.8 2.5 %collective-permute-start.8 = (bf16[3,2,16512]{2,1,0:T(2,128)(2,1)S(1)}, bf16[3,2,16512]{2,1,0:T(2,128)(2,1)S(1)}, u32[]{:S(2)}, u32[]{:S(2)}) collective-permute-start(bf16[3,2,16512]{2,1,0:T(2,128)(2,1)S(1)} %constant_dynamic-update-slice_fusion.refs_1_), channel_id=1, source_target_pairs={{0,6},{2,4},{4,2},{6,0},{8,14},{10,12},{12,10},{14,8},{16,22},{18,... | collective-permute-start | bytes 594440 | tf_op jit(solution)/shard_map/ppermute | solution.py:42
  16.3 0.5 collective-permute-start.6
  16.9 0.5 collective-permute-start.4
  17.4 2.4 %collective-permute-start.7 = (bf16[1,2,16512]{2,1,0:T(2,128)(2,1)S(1)}, bf16[1,2,16512]{2,1,0:T(2,128)(2,1)S(1)}, u32[]{:S(2)}, u32[]{:S(2)}) collective-permute-start(bf16[1,2,16512]{2,1,0:T(2,128)(2,1)S(1)} %bitcast.10), channel_id=1, source_target_pairs={{0,6},{2,4},{4,2},{6,0},{8,14},{10,12},{12,10},{14,8},{16,22},{18,... | collective-permute-start | bytes 198152 | tf_op jit(solution)/shard_map/ppermute | solution.py:42
  19.8 0.5 collective-permute-start.5
  20.3 7.1 %collective-permute-done.7.refs_6_ = bf16[1,2,16512]{2,1,0:T(2,128)(2,1)S(1)} collective-permute-done((bf16[1,2,16512]{2,1,0:T(2,128)(2,1)S(1)}, bf16[1,2,16512]{2,1,0:T(2,128)(2,1)S(1)}, u32[]{:S(2)}, u32[]{:S(2)}) %collective-permute-start.7) | collective-permute-done | bytes 66080 | tf_op jit(solution)/shard_map/ppermute | solution.py:42
  27.4 1.5 %collective-permute-start.3 = (bf16[1,2,16512]{2,1,0:T(2,128)(2,1)S(1)}, bf16[1,2,16512]{2,1,0:T(2,128)(2,1)S(1)}, u32[]{:S(2)}, u32[]{:S(2)}) collective-permute-start(bf16[1,2,16512]{2,1,0:T(2,128)(2,1)S(1)} %bitcast.12), channel_id=1, source_target_pairs={{0,2},{2,0},{4,6},{6,4},{8,10},{10,8},{12,14},{14,12},{16,18},{18,... | collective-permute-start | bytes 198152 | tf_op jit(solution)/shard_map/ppermute | solution.py:42
  28.9 3.4 %copy-done = bf16[64,128,512]{2,1,0:T(8,128)(2,1)S(1)} copy-done((bf16[64,128,512]{2,1,0:T(8,128)(2,1)S(1)}, bf16[64,128,512]{2,1,0:T(8,128)(2,1)}, u32[]{:S(2)}) %copy-start) | copy-done | bytes 8388632
  32.3 1.3 %copy-done.1 = bf16[576,1024]{1,0:T(8,128)(2,1)S(1)} copy-done((bf16[576,1024]{1,0:T(8,128)(2,1)S(1)}, bf16[576,1024]{1,0:T(8,128)(2,1)}, u32[]{:S(2)}) %copy-start.1) | copy-done | bytes 1179672
  33.6 0.9 %copy-done.2 = bf16[1024,128]{1,0:T(8,128)(2,1)S(1)} copy-done((bf16[1024,128]{1,0:T(8,128)(2,1)S(1)}, bf16[1024,128]{1,0:T(8,128)(2,1)}, u32[]{:S(2)}) %copy-start.2) | copy-done | bytes 262168
  34.5 0.8 %fetch.1 = (bf16[64,128,512]{2,1,0:T(8,128)(2,1)S(1)}, bf16[576,1024]{1,0:T(8,128)(2,1)S(1)}, bf16[1024,128]{1,0:T(8,128)(2,1)S(1)}) custom-call(bf16[64,128,512]{2,1,0:T(8,128)(2,1)S(1)} %copy-done, bf16[576,1024]{1,0:T(8,128)(2,1)S(1)} %copy-done.1, bf16[1024,128]{1,0:T(8,128)(2,1)S(1)} %copy-done.2), custom_call_target="tpu_custom_call" | custom-call | tf_op jit(solution)/shard_map/fetch/pallas_call | solution.py:255
  35.4 0.0 collective-permute-done.5.refs_4_
  35.4 0.0 collective-permute-done.3.refs_2_
  35.4 0.0 collective-permute-done.6.refs_5_
  35.4 0.0 collective-permute-done.4.refs_3_
  35.4 1.3 %index.1 = (bf16[32,16512]{1,0:T(8,128)(2,1)S(1)}, f32[32,32,1024]{2,1,0:T(8,128)S(1)}, f32[32,1024]{1,0:T(8,128)S(1)}, bf16[1024,128]{1,0:T(8,128)(2,1)S(1)}) custom-call(bf16[1024,128]{1,0:T(8,128)(2,1)S(1)} %get-tuple-element.20.key_ref, bf16[1,2,16512]{2,1,0:T(2,128)(2,1)S(1)} %bitcast.13, ...), custom_call_target="tpu_custom_call" | custom-call | tf_op jit(solution)/shard_map/index/pallas_call | solution.py:265
  36.8 0.1 collective-permute-start.9
  36.9 0.6 bias.1.bias_ref
  37.5 6.0 %scores.1 = (f32[64,32,1024]{2,1,0:T(8,128)S(1)}, f32[32,128]{1,0:T(8,128)S(1)}, f32[32,128]{1,0:T(8,128)S(1)}) custom-call(bf16[32,16512]{1,0:T(8,128)(2,1)S(1)} %get-tuple-element.22.rows_ref, bf16[64,128,512]{2,1,0:T(8,128)(2,1)S(1)} %get-tuple-element.23.w_ref, bf16[576,1024]{1,0:T(8,128)(2,1)S(1)} %get-tuple-element.24.latent_ref, ...), custom_call_target="tpu_custom_call" | custom-call | tf_op jit(solution)/shard_map/scores/pallas_call | solution.py:280
  43.5 0.0 collective-permute-done.9.other_ref
  43.5 0.4 stats.1
  43.9 11.8 %all_to_all.10.every_ref = f32[16,1,2176]{2,1,0:T(1,128)S(1)} all-to-all(f32[16,1,2176]{2,1,0:T(1,128)S(1)} %get-tuple-element.26), channel_id=1, replica_groups=mesh['ctx'=16,'head'=2] {'ctx'}, dimensions={0} | all-to-all | bytes 278528 | tf_op jit(solution)/shard_map/all_to_all | solution.py:306
  55.7 1.0 %target.1 = (f32[32,1024]{1,0:T(8,128)S(1)}, f32[32,1024]{1,0:T(8,128)S(1)}) custom-call(f32[16,1,2176]{2,1,0:T(1,128)S(1)} %all_to_all.10.every_ref, f32[32,128]{1,0:T(8,128)S(1)} %get-tuple-element.27.peak_ref, f32[32,128]{1,0:T(8,128)S(1)} %get-tuple-element.28.index_peak_ref, f32[64,32,1024]{2,1,0:T(8,128)S(1)} %get-tuple-element.29.power_ref, ...), custom_call_target="tpu_custom_call" | custom-call | tf_op jit(solution)/shard_map/target/pallas_call | solution.py:308
  56.7 0.1 collective-permute-start.10
  56.8 1.3 %collective-permute-done.10.other_ref = f32[32,1024]{1,0:T(8,128)S(1)} collective-permute-done((f32[32,1024]{1,0:T(8,128)S(1)}, f32[32,1024]{1,0:T(8,128)S(1)}, u32[]{:S(2)}, u32[]{:S(2)}) %collective-permute-start.10) | collective-permute-done | bytes 131104 | tf_op jit(solution)/shard_map/ppermute | solution.py:67
  58.1 1.6 %slopes.1 = (bf16[1024,1024]{1,0:T(8,128)(2,1)S(1)}, bf16[16,2,4096]{2,1,0:T(2,128)(2,1)}) custom-call(f32[32,1024]{1,0:T(8,128)S(1)} %get-tuple-element.31.predicted_ref, f32[32,1024]{1,0:T(8,128)S(1)} %get-tuple-element.32.target_ref, f32[32,1024]{1,0:T(8,128)S(1)} %collective-permute-done.10.other_ref, f32[32,32,1024]{2,1,0:T(8,128)S(1)} %get-tuple-element.33.gate_ref, ...), custom_call_target="tpu_custom_call" | custom-call | tf_op jit(solution)/shard_map/slopes/pallas_call | solution.py:318
  59.7 3.5 %all-to-all-start.1 = ((bf16[16,2,4096]{2,1,0:T(2,128)(2,1)}), bf16[16,2,4096]{2,1,0:T(2,128)(2,1)S(1)}, u32[]{:S(2)}, u32[]{:S(2)}) async-start(bf16[16,2,4096]{2,1,0:T(2,128)(2,1)} %get-tuple-element.34), calls=%async_computation.1 | async-start | bytes 524288 | tf_op jit(solution)/shard_map/all_to_all | solution.py:329
  63.3 0.0 copy-start.6
  63.3 0.0 copy-start.7
  63.3 0.7 fusion
  64.0 0.2 collective-permute-start.11
  64.2 9.4 %all-to-all-done.1 = bf16[16,2,4096]{2,1,0:T(2,128)(2,1)S(1)} async-done(((bf16[16,2,4096]{2,1,0:T(2,128)(2,1)}), bf16[16,2,4096]{2,1,0:T(2,128)(2,1)S(1)}, u32[]{:S(2)}, u32[]{:S(2)}) %all-to-all-start.1) | async-done | bytes 262176 | tf_op jit(solution)/shard_map/all_to_all | solution.py:329
  73.7 0.2 convert_reduce_fusion
  73.9 0.0 copy-start.5
  73.9 0.1 bitcast_reduce_fusion
  74.0 0.6 convert_divide_fusion
  74.6 0.8 %add.3 = f32[1024,128]{1,0:T(8,128)} add(f32[1024,128]{1,0:T(8,128)S(1)} %fusion, f32[1024,128]{1,0:T(8,128)S(1)} %collective-permute-done.11) | non-fusion elementwise | flops 131072 | bytes 1572864 | tf_op jit(solution)/shard_map/add | solution.py:334
  (13 shorter events, 0.1 us)
Async XLA Ops:
  1.6 5.7 %collective-permute-start = (bf16[1,2,16512]{2,1,0:T(2,128)(2,1)S(1)}, bf16[1,2,16512]{2,1,0:T(2,128)(2,1)S(1)}, u32[]{:S(2)}, u32[]{:S(2)}) collective-permute-start(bf16[1,2,16512]{2,1,0:T(2,128)(2,1)S(1)} %bitcast.7), channel_id=1, source_target_pairs={{0,8},{2,10},{4,12},{6,14},{8,0},{10,2},{12,4},{14,6},{16,24},{18,... | collective-permute-start | bytes 198152 | tf_op jit(solution)/shard_map/ppermute | solution.py:42
  4.7 9.0 %collective-permute-start.2 = (bf16[1,2,16512]{2,1,0:T(2,128)(2,1)S(1)}, bf16[1,2,16512]{2,1,0:T(2,128)(2,1)S(1)}, u32[]{:S(2)}, u32[]{:S(2)}) collective-permute-start(bf16[1,2,16512]{2,1,0:T(2,128)(2,1)S(1)} %bitcast.8), channel_id=1, source_target_pairs={{0,24},{2,26},{4,28},{6,30},{8,16},{10,18},{12,20},{14,22},{16,8},... | collective-permute-start | bytes 198152 | tf_op jit(solution)/shard_map/ppermute | solution.py:42
  7.2 6.5 %collective-permute-start.1 = (bf16[1,2,16512]{2,1,0:T(2,128)(2,1)S(1)}, bf16[1,2,16512]{2,1,0:T(2,128)(2,1)S(1)}, u32[]{:S(2)}, u32[]{:S(2)}) collective-permute-start(bf16[1,2,16512]{2,1,0:T(2,128)(2,1)S(1)} %bitcast.9), channel_id=1, source_target_pairs={{0,16},{2,18},{4,20},{6,22},{8,24},{10,26},{12,28},{14,30},{16,0},... | collective-permute-start | bytes 198152 | tf_op jit(solution)/shard_map/ppermute | solution.py:42
  13.7 23.1 %copy-start.3 = (s32[32]{0:T(128)S(1)}, s32[32]{0:T(128)}, u32[]{:S(2)}) copy-start(s32[32]{0:T(128)} %pos_ref.1) | copy-start | bytes 388
  13.8 23.1 %copy-start.4 = (s32[32]{0:T(128)S(1)}, s32[32]{0:T(128)}, u32[]{:S(2)}) copy-start(s32[32]{0:T(128)} %start_ref.1) | copy-start | bytes 388
  13.8 21.5 %collective-permute-start.8 = (bf16[3,2,16512]{2,1,0:T(2,128)(2,1)S(1)}, bf16[3,2,16512]{2,1,0:T(2,128)(2,1)S(1)}, u32[]{:S(2)}, u32[]{:S(2)}) collective-permute-start(bf16[3,2,16512]{2,1,0:T(2,128)(2,1)S(1)} %constant_dynamic-update-slice_fusion.refs_1_), channel_id=1, source_target_pairs={{0,6},{2,4},{4,2},{6,0},{8,14},{10,12},{12,10},{14,8},{16,22},{18,... | collective-permute-start | bytes 594440 | tf_op jit(solution)/shard_map/ppermute | solution.py:42
  16.3 19.0 %collective-permute-start.6 = (bf16[3,2,16512]{2,1,0:T(2,128)(2,1)S(1)}, bf16[3,2,16512]{2,1,0:T(2,128)(2,1)S(1)}, u32[]{:S(2)}, u32[]{:S(2)}) collective-permute-start(bf16[3,2,16512]{2,1,0:T(2,128)(2,1)S(1)} %constant_dynamic-update-slice_fusion.refs_1_), channel_id=1, source_target_pairs={{0,4},{2,6},{4,0},{6,2},{8,12},{10,14},{12,8},{14,10},{16,20},{18,... | collective-permute-start | bytes 594440 | tf_op jit(solution)/shard_map/ppermute | solution.py:42
  16.9 18.5 %collective-permute-start.4 = (bf16[3,2,16512]{2,1,0:T(2,128)(2,1)S(1)}, bf16[3,2,16512]{2,1,0:T(2,128)(2,1)S(1)}, u32[]{:S(2)}, u32[]{:S(2)}) collective-permute-start(bf16[3,2,16512]{2,1,0:T(2,128)(2,1)S(1)} %constant_dynamic-update-slice_fusion.refs_1_), channel_id=1, source_target_pairs={{0,2},{2,0},{4,6},{6,4},{8,10},{10,8},{12,14},{14,12},{16,18},{18,... | collective-permute-start | bytes 594440 | tf_op jit(solution)/shard_map/ppermute | solution.py:42
  17.4 10.0 %collective-permute-start.7 = (bf16[1,2,16512]{2,1,0:T(2,128)(2,1)S(1)}, bf16[1,2,16512]{2,1,0:T(2,128)(2,1)S(1)}, u32[]{:S(2)}, u32[]{:S(2)}) collective-permute-start(bf16[1,2,16512]{2,1,0:T(2,128)(2,1)S(1)} %bitcast.10), channel_id=1, source_target_pairs={{0,6},{2,4},{4,2},{6,0},{8,14},{10,12},{12,10},{14,8},{16,22},{18,... | collective-permute-start | bytes 198152 | tf_op jit(solution)/shard_map/ppermute | solution.py:42
  19.8 15.5 %collective-permute-start.5 = (bf16[1,2,16512]{2,1,0:T(2,128)(2,1)S(1)}, bf16[1,2,16512]{2,1,0:T(2,128)(2,1)S(1)}, u32[]{:S(2)}, u32[]{:S(2)}) collective-permute-start(bf16[1,2,16512]{2,1,0:T(2,128)(2,1)S(1)} %bitcast.11), channel_id=1, source_target_pairs={{0,4},{2,6},{4,0},{6,2},{8,12},{10,14},{12,8},{14,10},{16,20},{18,... | collective-permute-start | bytes 198152 | tf_op jit(solution)/shard_map/ppermute | solution.py:42
  27.4 8.0 %collective-permute-start.3 = (bf16[1,2,16512]{2,1,0:T(2,128)(2,1)S(1)}, bf16[1,2,16512]{2,1,0:T(2,128)(2,1)S(1)}, u32[]{:S(2)}, u32[]{:S(2)}) collective-permute-start(bf16[1,2,16512]{2,1,0:T(2,128)(2,1)S(1)} %bitcast.12), channel_id=1, source_target_pairs={{0,2},{2,0},{4,6},{6,4},{8,10},{10,8},{12,14},{14,12},{16,18},{18,... | collective-permute-start | bytes 198152 | tf_op jit(solution)/shard_map/ppermute | solution.py:42
  28.9 3.4 %copy-start = (bf16[64,128,512]{2,1,0:T(8,128)(2,1)S(1)}, bf16[64,128,512]{2,1,0:T(8,128)(2,1)}, u32[]{:S(2)}) copy-start(bf16[64,128,512]{2,1,0:T(8,128)(2,1)} %refs_0_.1) | copy-start | bytes 25165828
  32.3 1.3 %copy-start.1 = (bf16[576,1024]{1,0:T(8,128)(2,1)S(1)}, bf16[576,1024]{1,0:T(8,128)(2,1)}, u32[]{:S(2)}) copy-start(bf16[576,1024]{1,0:T(8,128)(2,1)} %refs_1_.1) | copy-start | bytes 3538948
  33.5 0.9 %copy-start.2 = (bf16[1024,128]{1,0:T(8,128)(2,1)S(1)}, bf16[1024,128]{1,0:T(8,128)(2,1)}, u32[]{:S(2)}) copy-start(bf16[1024,128]{1,0:T(8,128)(2,1)} %refs_2_.1) | copy-start | bytes 786436
  36.8 6.7 %collective-permute-start.9 = (f32[32,1024]{1,0:T(8,128)S(1)}, f32[32,1024]{1,0:T(8,128)S(1)}, u32[]{:S(2)}, u32[]{:S(2)}) collective-permute-start(f32[32,1024]{1,0:T(8,128)S(1)} %get-tuple-element.21.part_ref), channel_id=1, source_target_pairs={{0,1},{1,0},{2,3},{3,2},{4,5},{5,4},{6,7},{7,6},{8,9},{9,8},{10,11... | collective-permute-start | bytes 393224 | tf_op jit(solution)/shard_map/ppermute | solution.py:67
  56.7 1.4 %collective-permute-start.10 = (f32[32,1024]{1,0:T(8,128)S(1)}, f32[32,1024]{1,0:T(8,128)S(1)}, u32[]{:S(2)}, u32[]{:S(2)}) collective-permute-start(f32[32,1024]{1,0:T(8,128)S(1)} %get-tuple-element.32.target_ref), channel_id=1, source_target_pairs={{0,1},{1,0},{2,3},{3,2},{4,5},{5,4},{6,7},{7,6},{8,9},{9,8},{10,11... | collective-permute-start | bytes 393224 | tf_op jit(solution)/shard_map/ppermute | solution.py:67
  59.7 13.9 %all-to-all-start.1 = ((bf16[16,2,4096]{2,1,0:T(2,128)(2,1)}), bf16[16,2,4096]{2,1,0:T(2,128)(2,1)S(1)}, u32[]{:S(2)}, u32[]{:S(2)}) async-start(bf16[16,2,4096]{2,1,0:T(2,128)(2,1)} %get-tuple-element.34), calls=%async_computation.1 | async-start | bytes 524288 | tf_op jit(solution)/shard_map/all_to_all | solution.py:329
  63.3 10.6 %copy-start.6 = (bf16[2,4096]{1,0:T(2,128)(2,1)S(1)}, bf16[2,4096]{1,0:T(2,128)(2,1)}, u32[]{:S(2)}) copy-start(bf16[2,4096]{1,0:T(2,128)(2,1)} %param.11) | copy-start | bytes 49156
  63.3 10.7 %copy-start.7 = (bf16[2,32]{1,0:T(2,128)(2,1)S(1)}, bf16[2,32]{1,0:T(2,128)(2,1)}, u32[]{:S(2)}) copy-start(bf16[2,32]{1,0:T(2,128)(2,1)} %param.13) | copy-start | bytes 388
  64.0 10.6 %collective-permute-start.11 = (f32[1024,128]{1,0:T(8,128)S(1)}, f32[1024,128]{1,0:T(8,128)S(1)}, u32[]{:S(2)}, u32[]{:S(2)}) collective-permute-start(f32[1024,128]{1,0:T(8,128)S(1)} %fusion), channel_id=1, source_target_pairs={{0,1},{1,0},{2,3},{3,2},{4,5},{5,4},{6,7},{7,6},{8,9},{9,8},{10,11... | collective-permute-start | bytes 1572872 | tf_op jit(solution)/shard_map/ppermute | solution.py:67
  73.9 1.6 %copy-start.5 = (f32[2,4096]{1,0:T(2,128)}, f32[2,4096]{1,0:T(2,128)S(1)}, u32[]{:S(2)}) copy-start(f32[2,4096]{1,0:T(2,128)S(1)} %convert_reduce_fusion) | copy-start | bytes 98308
